TPU v7x, 128 devices: a whole 4x4x4 slice. The times are simulated.
128 devices in a mesh: expert: 8 (over z, core), fsdp: 16 (over y, x).
Axes of the slice: x: 4, y: 4, z: 4, core: 2. Of those that a mesh axis runs over, the one named last changes fastest.
Arguments:
- hidden: bfloat16 [8, 768, 8192], P('expert', None, 'fsdp'), may hold values from -0.198873782 to 0.198873782
- expert_ids: int32 [2048, 2], P(('expert', 'fsdp')), may hold values from 0 to 7, all different within a row; in each aligned block of 16 rows (0 to 15, 16 to 31, ...) at most 6 rows name the same one
- gate_weights: float32 [2048, 2], P(('expert', 'fsdp')), may hold values from 0.2 to 1
- loss_weight: float32 [2048], P(('expert', 'fsdp')), may hold values from 0.3 to 3
- decay: float32 [1], replicated, may hold values from 0.2 to 0.6
- val_grad: bfloat16 [8, 8192, 4096], P('expert', 'fsdp'), may hold values from -8 to 8
- down_weight: bfloat16 [8, 8192, 4096], P('expert', 'fsdp'), may hold values from -0.0625 to 0.0625
Outputs:
- solution: float32 [8, 8192, 4096], P('expert', 'fsdp')
- hyper: float32 [1], replicated
Inputs may be any that keep to these rules, and one draw needn't show every extreme that they name: `expert_ids`: each token names 2 different experts; among the 16 tokens of one device no expert is named more than 6 times, a bound that some block reaches.
All inputs are finite; a program needn't handle non-finite values.
Results may differ from a plain program's by a relative error of at most 0.00067.
Values may be sent and summed in bfloat16 or wider, within the bound.
No kernel may reach another device: no remote copies, remote signals or barrier semaphores. Data moves between devices by JAX's collectives and lax.ppermute only.
A program may use at most 128 MiB of HBM per device.

v0:
```python
import math
import jax
import jax.numpy as jnp
from jax import lax
from jax.sharding import Mesh
from jax.sharding import PartitionSpec as P

D = 4096
ITERS = 2
EXPERT_FSDP = ("expert_0", "expert_1", "fsdp_0", "fsdp_1")
EXPERT = ("expert_0", "expert_1")
FSDP = ("fsdp_0", "fsdp_1")


def by_axis(array, axes):
    for axis in axes:
        array = lax.psum(array, axis)
    return array


def gate_table(expert_ids, gate_weights, experts, capacity):
    flat_ids = expert_ids.reshape(-1)
    labels = jnp.arange(experts, dtype=jnp.int32)
    onehot = (flat_ids[:, None] == labels[None, :]).astype(jnp.int32)
    earlier = jnp.cumsum(onehot, axis=0) - onehot
    slots = jnp.sum(earlier * onehot, axis=1)
    targets = flat_ids * capacity + slots
    columns = jnp.arange(experts * capacity, dtype=jnp.int32)
    hits = (targets[:, None] == columns[None, :]).astype(jnp.float32)
    weighted = hits * gate_weights.reshape(-1)[:, None]
    return jnp.sum(weighted.reshape(-1, expert_ids.shape[1], experts * capacity), axis=1)


def combine(table, weights, outputs):
    mixed = jnp.dot(
        table, outputs, precision=lax.Precision.HIGHEST, preferred_element_type=jnp.float32
    )
    scaled = weights[:, None] * mixed
    back = jnp.dot(
        table.T, scaled, precision=lax.Precision.HIGHEST, preferred_element_type=jnp.float32
    )
    return back.astype(jnp.bfloat16)


def joined_sums(residual, direction, image, target):
    return (
        by_axis(jnp.sum(residual * residual), EXPERT_FSDP),
        by_axis(jnp.sum(direction * image), EXPERT_FSDP),
        by_axis(jnp.sum(residual * image), EXPERT_FSDP),
        by_axis(jnp.sum(image * image), EXPERT_FSDP),
        by_axis(jnp.sum(target.astype(jnp.float32) * direction), EXPERT_FSDP),
    )


def local(hidden, expert_ids, gate_weights, loss_weight, decay, val_grad, down_weight):
    n_expert = lax.axis_size(EXPERT)
    n_fsdp = lax.axis_size(FSDP)
    capacity = hidden.shape[1] // (n_expert * n_fsdp)
    decay_rate = decay[0]
    table = gate_table(expert_ids, gate_weights, n_expert, capacity)
    local_hidden = hidden[0]
    right_side, target = (val_grad, down_weight)
    start_side = right_side.astype(jnp.float32)
    solution = jnp.zeros_like(start_side)
    residual = start_side
    direction = start_side
    along_total = jnp.float32(0.0)
    for iteration in range(ITERS):
        if iteration > 0:
            direction = residual + norm_guess / norm_prev * direction
        rounded = direction[0].astype(jnp.bfloat16)
        summed = lax.psum_scatter(
            jnp.dot(local_hidden, rounded, preferred_element_type=jnp.float32),
            FSDP,
            scatter_dimension=0,
            tiled=True,
        )
        arrived = lax.all_to_all(summed, EXPERT, split_axis=0, concat_axis=0, tiled=True)
        leaving = combine(table, loss_weight, arrived)
        returned = lax.all_to_all(leaving, EXPERT, split_axis=0, concat_axis=0, tiled=True)
        gradient = lax.dot_general(
            local_hidden,
            lax.all_gather(returned, FSDP, axis=0, tiled=True),
            (((0,), (0,)), ((), ())),
            preferred_element_type=jnp.float32,
        )
        image = gradient[None] + decay_rate * direction
        norm_now, curve, cross, square, along = joined_sums(residual, direction, image, target)
        alpha = norm_now / curve
        solution = solution + alpha * direction
        residual = residual - alpha * image
        norm_guess = norm_now - 2.0 * alpha * cross + alpha * alpha * square
        norm_prev = norm_now
        along_total = along_total + alpha * along
    hyper = -along_total / math.sqrt(n_expert * D)
    return (solution, jnp.reshape(hyper, (1,)))


def solution(mesh):
    finer = Mesh(mesh.devices.reshape(4, 2, 4, 4), ("expert_0", "expert_1", "fsdp_0", "fsdp_1"))
    placed = (
        P(EXPERT, None, FSDP),
        P(EXPERT_FSDP, None),
        P(EXPERT_FSDP, None),
        P(EXPERT_FSDP),
        P(),
        P(EXPERT, FSDP, None),
        P(EXPERT, FSDP, None),
    )
    return jax.shard_map(
        local, mesh=finer, in_specs=placed, out_specs=(P(EXPERT, FSDP, None), P()), check_vma=False
    )
```

profile of v0, /device:TPU:0, one launch (start us, length us, event | category | flops | bytes accessed | tf_op | source)
XLA Modules:
  0.0 544.2 jit_solution(16271983358100491739)
XLA Ops:
  7.2 0.0 copy-start
  7.2 0.0 reduce-scatter.5.cloned.1.call-start
  7.2 1.1 copy-done
  8.3 8.6 %fusion.10 = f32[768,4096]{1,0:T(8,128)} fusion(bf16[1,512,4096]{2,1,0:T(8,128)(2,1)} %param.12, bf16[1,768,512]{2,1,0:T(8,128)(2,1)S(1)} %copy-done), kind=kOutput, calls=%fused_computation.26 | convolution fusion | flops 3221225472 | bytes 17563648 | tf_op jit(solution)/shard_map/dot_general | solution.py:73
  16.9 0.0 copy-start.1
  16.9 0.0 copy-start.3
  16.9 0.0 copy-start.2
  16.9 0.0 reduce-scatter.5.cloned.1.call-update
  16.9 97.7 %reduce-scatter.5.cloned.1.call-done = f32[48,4096]{1,0:T(8,128)} async-done(((f32[768,4096]{1,0:T(8,128)}), f32[48,4096]{1,0:T(8,128)}) %reduce-scatter.5.cloned.1.call-update) | async-done | bytes 786448 | tf_op jit(solution)/shard_map/reduce_scatter | solution.py:72
  114.5 2.2 all_to_all.32
  116.7 4.4 all-to-all-start
  121.2 0.0 all-gather.3.cloned.1.call-start
  121.2 0.0 copy-done.1
  121.2 0.1 copy.41
  121.3 0.1 eq.29
  121.4 0.1 fusion.17
  121.5 0.1 reduce_window_sum.11
  121.5 0.2 select_reduce_fusion.1
  121.7 0.1 reduce_sum.89
  121.8 0.1 copy.42
  121.9 0.0 copy-done.3
  121.9 0.1 select_reduce_fusion
  122.0 15.1 %all-to-all-done = f32[8,6,4096]{2,1,0:T(8,128)S(1)} async-done(((f32[8,6,4096]{2,1,0:T(8,128)}), f32[8,6,4096]{2,1,0:T(8,128)S(1)}, u32[]{:S(2)}, u32[]{:S(2)}) %all-to-all-start) | async-done | bytes 786464 | tf_op jit(solution)/shard_map/all_to_all | solution.py:78
  137.1 0.1 all_to_all.34
  137.2 0.0 copy-done.2
  137.2 0.5 convolution_multiply_fusion.1
  137.7 0.8 convolution_convert_fusion.1
  138.6 0.1 all_to_all.35
  138.7 12.8 %all_to_all.48 = bf16[8,6,4096]{2,1,0:T(8,128)(2,1)S(1)} all-to-all(bf16[8,6,4096]{2,1,0:T(8,128)(2,1)S(1)} %all_to_all.35), channel_id=1, replica_groups=mesh['expert_0'=4,'expert_1'=2,'fsdp_0'=4,'fsdp_1'=4] {'expert_0','exper..., dimensions={0} | all-to-all | bytes 786432 | tf_op jit(solution)/shard_map/all_to_all | solution.py:80
  151.5 0.9 all_to_all.37
  152.3 0.0 all-gather.3.cloned.1.call-update
  152.4 0.0 reduce-scatter.7.cloned.1.call-start
  152.4 6.5 %copy.40 = bf16[1,512,4096]{1,2,0:T(8,128)(2,1)} copy(bf16[1,512,4096]{2,1,0:T(8,128)(2,1)} %param.12) | data formatting | bytes 8388608 | tf_op args[5]
  159.6 51.1 %all-gather.3.cloned.1.call-done = bf16[768,4096]{1,0:T(8,128)(2,1)} async-done(((bf16[48,4096]{1,0:T(8,128)(2,1)}), bf16[768,4096]{1,0:T(8,128)(2,1)}) %all-gather.3.cloned.1.call-update) | async-done | bytes 6291472 | tf_op jit(solution)/shard_map/all_gather | solution.py:83
  210.7 12.3 %multiply_reduce_fusion = (f32[]{:T(128)}, f32[]{:T(128)}, f32[]{:T(128)}, f32[1,512,4096]{1,2,0:T(8,128)}) fusion(bf16[1,512,4096]{1,2,0:T(8,128)(2,1)} %copy.40, f32[]{:T(128)} %bitcast.44, bf16[768,4096]{1,0:T(8,128)(2,1)} %all-gather.3.cloned.1.call-done, bf16[1,768,512]{2,1,0:T(8,128)(2,1)S(1)} %copy-done), kind=kOutput, calls=%fused_computation.18 | convolution fusion | flops 3240099840 | bytes 19660816 | tf_op jit(solution)/shard_map/dot_general | solution.py:81
  222.9 11.4 %all-reduce.5 = (f32[]{:T(128)}, f32[]{:T(128)}, f32[]{:T(128)}) all-reduce(f32[]{:T(128)} %get-tuple-element.17, f32[]{:T(128)} %get-tuple-element.16, f32[]{:T(128)} %get-tuple-element.15), channel_id=1, replica_groups=mesh['expert_0'=4,'expert_1'=2,'fsdp_0'=4,'fsdp_1'=4] {'expert_0'}, use_global_device_ids=true, to_apply=%region_1.2 | all-reduce | flops 3 | bytes 24 | tf_op jit(solution)/shard_map/psum | solution.py:17
  234.3 3.1 all-reduce.7
  237.4 11.1 %all-reduce.3 = (f32[]{:T(128)}, f32[]{:T(128)}, f32[]{:T(128)}) all-reduce(f32[]{:T(128)} %get-tuple-element.43, f32[]{:T(128)} %get-tuple-element.44, f32[]{:T(128)} %get-tuple-element.45), channel_id=1, replica_groups=mesh['expert_0'=4,'expert_1'=2,'fsdp_0'=4,'fsdp_1'=4] {'fsdp_0'}, use_global_device_ids=true, to_apply=%region_3.4 | all-reduce | flops 3 | bytes 24 | tf_op jit(solution)/shard_map/psum | solution.py:17
  248.5 9.4 %all-reduce.1 = (f32[]{:T(128)}, f32[]{:T(128)}, f32[]{:T(128)}) all-reduce(f32[]{:T(128)} %get-tuple-element.29, f32[]{:T(128)} %get-tuple-element.30, f32[]{:T(128)} %get-tuple-element.31), channel_id=1, replica_groups=mesh['expert_0'=4,'expert_1'=2,'fsdp_0'=4,'fsdp_1'=4] {'fsdp_1'}, use_global_device_ids=true, to_apply=%region_4.5 | all-reduce | flops 3 | bytes 24 | tf_op jit(solution)/shard_map/psum | solution.py:17
  261.8 13.1 %convolution_bitcast_fusion = f32[768,4096]{0,1:T(8,128)} fusion(bf16[1,768,512]{2,1,0:T(8,128)(2,1)S(1)} %copy-done, bf16[1,512,4096]{1,2,0:T(8,128)(2,1)} %copy.40, f32[1,512,4096]{1,2,0:T(8,128)} %get-tuple-element.46, f32[]{:T(128)S(6)} %div.13, f32[]{:T(128)S(6)} %div.12), kind=kOutput, calls=%fused_computation.20 | convolution fusion | flops 3233808384 | bytes 25952264 | tf_op jit(solution)/shard_map/dot_general | solution.py:73
  274.9 12.6 %copy.46 = f32[768,4096]{1,0:T(8,128)} copy(f32[768,4096]{0,1:T(8,128)} %convolution_bitcast_fusion) | data formatting | bytes 25165824
  287.5 0.0 reduce-scatter.7.cloned.1.call-update
  287.5 0.0 all-gather.5.cloned.1.call-start
  287.6 89.8 %reduce-scatter.7.cloned.1.call-done = f32[48,4096]{1,0:T(8,128)} async-done(((f32[768,4096]{1,0:T(8,128)}), f32[48,4096]{1,0:T(8,128)}) %reduce-scatter.7.cloned.1.call-update) | async-done | bytes 786448 | tf_op jit(solution)/shard_map/reduce_scatter | solution.py:72
  377.4 1.2 all_to_all.38
  378.6 20.2 %all_to_all.49 = f32[8,6,4096]{2,1,0:T(8,128)S(1)} all-to-all(f32[8,6,4096]{2,1,0:T(8,128)S(1)} %all_to_all.38), channel_id=1, replica_groups=mesh['expert_0'=4,'expert_1'=2,'fsdp_0'=4,'fsdp_1'=4] {'expert_0','exper..., dimensions={0} | all-to-all | bytes 1572864 | tf_op jit(solution)/shard_map/all_to_all | solution.py:78
  398.8 0.1 all_to_all.40
  398.9 0.5 convolution_multiply_fusion
  399.4 0.8 convolution_convert_fusion
  400.2 0.1 all_to_all.41
  400.4 12.8 %all_to_all.50 = bf16[8,6,4096]{2,1,0:T(8,128)(2,1)S(1)} all-to-all(bf16[8,6,4096]{2,1,0:T(8,128)(2,1)S(1)} %all_to_all.41), channel_id=1, replica_groups=mesh['expert_0'=4,'expert_1'=2,'fsdp_0'=4,'fsdp_1'=4] {'expert_0','exper..., dimensions={0} | all-to-all | bytes 786432 | tf_op jit(solution)/shard_map/all_to_all | solution.py:80
  413.1 0.9 all_to_all.43
  414.1 0.0 all-gather.5.cloned.1.call-update
  414.1 6.6 %copy.44 = bf16[1,512,4096]{1,2,0:T(8,128)(2,1)} copy(bf16[1,512,4096]{2,1,0:T(8,128)(2,1)} %param.13) | data formatting | bytes 8388608 | tf_op args[6]
  420.7 8.4 %fusion = (f32[]{:T(128)}, f32[]{:T(128)}, f32[]{:T(128)}) fusion(bf16[1,512,4096]{1,2,0:T(8,128)(2,1)} %copy.44, f32[]{:T(128)S(6)} %div.13, f32[1,512,4096]{1,2,0:T(8,128)} %get-tuple-element.46, f32[]{:T(128)S(6)} %div.12, bf16[1,512,4096]{1,2,0:T(8,128)(2,1)} %copy.40), kind=kLoop, calls=%fused_computation.8 | loop fusion | flops 25165824 | bytes 16777236 | tf_op jit(solution)/shard_map/reduce_sum | solution.py:51
  429.0 43.4 %all-gather.5.cloned.1.call-done = bf16[768,4096]{1,0:T(8,128)(2,1)} async-done(((bf16[48,4096]{1,0:T(8,128)(2,1)}), bf16[768,4096]{1,0:T(8,128)(2,1)}) %all-gather.5.cloned.1.call-update) | async-done | bytes 6291472 | tf_op jit(solution)/shard_map/all_gather | solution.py:83
  472.4 10.1 %fusion.8 = f32[]{:T(128)} fusion(bf16[768,4096]{1,0:T(8,128)(2,1)} %all-gather.5.cloned.1.call-done, f32[]{:T(128)} %bitcast.45, bf16[1,768,512]{2,1,0:T(8,128)(2,1)S(1)} %copy-done, f32[]{:T(128)S(6)} %div.13, f32[1,512,4096]{1,2,0:T(8,128)} %get-tuple-element.46, f32[]{:T(128)S(6)} %div.12, bf16[1,512,4096]{1,2,0:T(8,128)(2,1)} %copy.40), kind=kOutput, calls=%fused_computation.17 | convolution fusion | flops 3240099840 | bytes 19660816 | tf_op jit(solution)/shard_map/dot_general | solution.py:81
  482.5 11.4 %all-reduce.4 = (f32[]{:T(128)}, f32[]{:T(128)}, f32[]{:T(128)}, f32[]{:T(128)}) all-reduce(f32[]{:T(128)} %get-tuple-element.13, f32[]{:T(128)} %fusion.8, f32[]{:T(128)} %get-tuple-element.14, f32[]{:T(128)} %get-tuple-element.12), channel_id=1, replica_groups=mesh['expert_0'=4,'expert_1'=2,'fsdp_0'=4,'fsdp_1'=4] {'expert_0'}, use_global_device_ids=true, to_apply=%region_15.16 | all-reduce | flops 4 | bytes 32 | tf_op jit(solution)/shard_map/psum | solution.py:17
  493.9 3.2 all-reduce.6
  497.0 11.1 %all-reduce.2 = (f32[]{:T(128)}, f32[]{:T(128)}, f32[]{:T(128)}, f32[]{:T(128)}) all-reduce(f32[]{:T(128)} %get-tuple-element.39, f32[]{:T(128)} %get-tuple-element.40, f32[]{:T(128)} %get-tuple-element.41, f32[]{:T(128)} %get-tuple-element.42), channel_id=1, replica_groups=mesh['expert_0'=4,'expert_1'=2,'fsdp_0'=4,'fsdp_1'=4] {'fsdp_0'}, use_global_device_ids=true, to_apply=%region_17.18 | all-reduce | flops 4 | bytes 32 | tf_op jit(solution)/shard_map/psum | solution.py:17
  508.1 9.2 %all-reduce = (f32[]{:T(128)}, f32[]{:T(128)}, f32[]{:T(128)}, f32[]{:T(128)}) all-reduce(f32[]{:T(128)} %get-tuple-element.25, f32[]{:T(128)} %get-tuple-element.26, f32[]{:T(128)} %get-tuple-element.27, f32[]{:T(128)} %get-tuple-element.28), channel_id=1, replica_groups=mesh['expert_0'=4,'expert_1'=2,'fsdp_0'=4,'fsdp_1'=4] {'fsdp_1'}, use_global_device_ids=true, to_apply=%region_18.19 | all-reduce | flops 4 | bytes 32 | tf_op jit(solution)/shard_map/psum | solution.py:17
  518.7 7.7 %fusion.4 = f32[1,512,4096]{1,2,0:T(8,128)} fusion(bf16[1,512,4096]{1,2,0:T(8,128)(2,1)} %copy.40, f32[]{:T(128)S(6)} %div.14, f32[]{:T(128)S(6)} %div.12, f32[]{:T(128)S(6)} %div.13, f32[1,512,4096]{1,2,0:T(8,128)} %get-tuple-element.46), kind=kLoop, calls=%fused_computation.12 | loop fusion | flops 16777216 | bytes 20971532 | tf_op jit(solution)/shard_map/add | solution.py:90
  527.6 8.9 %copy.45 = f32[1,512,4096]{2,1,0:T(8,128)} copy(f32[1,512,4096]{1,2,0:T(8,128)} %fusion.4) | data formatting | bytes 16777216
  (1 shorter events, 0.0 us)
Async XLA Ops:
  7.2 1.1 copy-start
  7.2 107.4 %reduce-scatter.5.cloned.1.call-start = ((), (), s32[]{:S(2)}) async-start(), calls=%async_computation.6 | async-start | bytes 13369344 | tf_op jit(solution)/shard_map/reduce_scatter | solution.py:72
  16.9 104.4 %copy-start.1 = (s32[16,2]{0,1:T(2,128)S(1)}, s32[16,2]{0,1:T(2,128)}, u32[]{:S(2)}) copy-start(s32[16,2]{0,1:T(2,128)} %param.8) | copy-start | bytes 388
  16.9 105.0 %copy-start.3 = (f32[16,2]{0,1:T(2,128)S(1)}, f32[16,2]{0,1:T(2,128)}, u32[]{:S(2)}) copy-start(f32[16,2]{0,1:T(2,128)} %param.9) | copy-start | bytes 388
  16.9 120.4 %copy-start.2 = (f32[16]{0:T(128)S(1)}, f32[16]{0:T(128)}, u32[]{:S(2)}) copy-start(f32[16]{0:T(128)} %param.10) | copy-start | bytes 196
  116.7 20.4 %all-to-all-start = ((f32[8,6,4096]{2,1,0:T(8,128)}), f32[8,6,4096]{2,1,0:T(8,128)S(1)}, u32[]{:S(2)}, u32[]{:S(2)}) async-start(f32[8,6,4096]{2,1,0:T(8,128)} %all_to_all.32), calls=%async_computation.1 | async-start | bytes 2097152 | tf_op jit(solution)/shard_map/all_to_all | solution.py:78
  121.2 89.5 %all-gather.3.cloned.1.call-start = ((), (), s32[]{:S(2)}) async-start(), calls=%async_computation.7 | async-start | bytes 6684672 | tf_op jit(solution)/shard_map/all_gather | solution.py:83
  152.4 225.0 %reduce-scatter.7.cloned.1.call-start = ((), (), s32[]{:S(2)}) async-start(), calls=%async_computation.9 | async-start | bytes 13369344 | tf_op jit(solution)/shard_map/reduce_scatter | solution.py:72
  287.5 184.9 %all-gather.5.cloned.1.call-start = ((), (), s32[]{:S(2)}) async-start(), calls=%async_computation.8 | async-start | bytes 6684672 | tf_op jit(solution)/shard_map/all_gather | solution.py:83
Sparse Core Ops, SparseCore 0:
  17.0 97.4 reduce-scatter.4
  152.5 58.1 all-gather.2
  287.6 89.6 reduce-scatter.6
  414.2 58.1 all-gather.4
where the time goes:
time: 545 us; the launch traced here: 544 us
  waiting for transfers between devices  297 us (54%)
  blocking collectives  116 us (21%)
  matrix products  46.6 us (9%)
  local copies, waits for them, and re-layouts  41.8 us (8%)
  between operations  22 us (4%)
  other arithmetic  16.5 us (3%)
    reduce_scatter x2, waiting for transfers between devices, local(): lax.psum_scatter(jnp.dot(local_hidden, rounded, preferred_element_type=jn...  187 us
    all_gather x2, waiting for transfers between devices, local(): lax.all_gather(returned, FSDP, axis=0, tiled=True)  94.5 us
    psum x8, blocking collectives, by_axis(): array = lax.psum(array, axis)  69.9 us
    unnamed x13, local copies, waits for them, and re-layouts  35.8 us
    all_to_all x2, blocking collectives, local(): lax.all_to_all(leaving, EXPERT, split_axis=0, concat_axis=0, tiled=True)  25.5 us
    dot_general x2, matrix products, local(): lax.dot_general(local_hidden, lax.all_gather(returned, FSDP, axis=0, tile...  22.3 us
    dot_general x2, matrix products, local(): jnp.dot(local_hidden, rounded, preferred_element_type=jnp.float32)  21.6 us
    all_to_all x1, blocking collectives, local(): lax.all_to_all(summed, EXPERT, split_axis=0, concat_axis=0, tiled=True)  20.2 us
  transfers between devices with their start and end apart: 5, of which 5 were waited for; matrix products, arithmetic and copies ran while one was open for 4% of the time, Pallas kernels for 0%

commit v1 on v0

--- a/solution.py
+++ b/solution.py
@@ -80,7 +80,9 @@
         returned = lax.all_to_all(leaving, EXPERT, split_axis=0, concat_axis=0, tiled=True)
         gradient = lax.dot_general(
             local_hidden,
-            lax.all_gather(returned, FSDP, axis=0, tiled=True),
+            jnp.concatenate(
+                lax.all_to_all(jnp.stack([returned] * lax.psum(1, FSDP)), FSDP, 0, 0), axis=0
+            ),
             (((0,), (0,)), ((), ())),
             preferred_element_type=jnp.float32,
         )

time: 545 us -> 626 us (1.15)
  waiting for transfers between devices: 297 us -> 367 us
  starting transfers between devices: 4.58 us -> 13.8 us
    all_to_all x0 -> x2, waiting for transfers between devices: none -> 164 us  [local(): lax.all_to_all(jnp.stack([returned] * lax.psum(1, FSDP)), FSDP, 0, 0)]
    all_gather x2 -> x0, waiting for transfers between devices: 94.5 us -> none  [local(): lax.all_gather(returned, FSDP, axis=0, tiled=True)]
    all_to_all x0 -> x2, starting transfers between devices: none -> 9.26 us  [local(): lax.all_to_all(jnp.stack([returned] * lax.psum(1, FSDP)), FSDP, 0, 0)]
    another operation x0 -> x4, local copies, waits for them, and re-layouts: none -> 7.18 us  [local(): jnp.stack([returned] * lax.psum(1, FSDP))]
where the time goes in v1:
time: 626 us; the launch traced here: 625 us
  waiting for transfers between devices  367 us (59%)
  blocking collectives  112 us (18%)
  local copies, waits for them, and re-layouts  47.1 us (8%)
  matrix products  46.7 us (7%)
  between operations  22.3 us (4%)
  other arithmetic  16.3 us (3%)
  starting transfers between devices  13.8 us (2%)
    reduce_scatter x2, waiting for transfers between devices, local(): lax.psum_scatter(jnp.dot(local_hidden, rounded, preferred_element_type=jn...  188 us
    all_to_all x2, waiting for transfers between devices, local(): lax.all_to_all(jnp.stack([returned] * lax.psum(1, FSDP)), FSDP, 0, 0)  164 us
    psum x8, blocking collectives, by_axis(): array = lax.psum(array, axis)  66.1 us
    unnamed x13, local copies, waits for them, and re-layouts  35.7 us
    all_to_all x2, blocking collectives, local(): lax.all_to_all(leaving, EXPERT, split_axis=0, concat_axis=0, tiled=True)  25.5 us
    dot_general x2, matrix products, local(): lax.dot_general(local_hidden, jnp.concatenate(lax.all_to_all(jnp.stack([r...  22.4 us
    dot_general x2, matrix products, local(): jnp.dot(local_hidden, rounded, preferred_element_type=jnp.float32)  21.6 us
    all_to_all x1, blocking collectives, local(): lax.all_to_all(summed, EXPERT, split_axis=0, concat_axis=0, tiled=True)  20.2 us
  transfers between devices with their start and end apart: 5, of which 5 were waited for; matrix products, arithmetic and copies ran while one was open for 4% of the time, Pallas kernels for 0%

profile of v1, /device:TPU:0, one launch (start us, length us, event | category | flops | bytes accessed | tf_op | source)
XLA Modules:
  0.0 625.0 jit_solution(17462206237105110553)
XLA Ops:
  7.2 0.0 copy-start
  7.2 0.0 reduce-scatter.5.cloned.1.call-start
  7.2 1.1 copy-done
  8.3 8.6 %fusion.10 = f32[768,4096]{1,0:T(8,128)} fusion(bf16[1,512,4096]{2,1,0:T(8,128)(2,1)} %param.12, bf16[1,768,512]{2,1,0:T(8,128)(2,1)S(1)} %copy-done), kind=kOutput, calls=%fused_computation.26 | convolution fusion | flops 3221225472 | bytes 17563648 | tf_op jit(solution)/shard_map/dot_general | solution.py:73
  16.9 0.0 copy-start.1
  16.9 0.0 copy-start.3
  16.9 0.0 copy-start.2
  16.9 0.0 reduce-scatter.5.cloned.1.call-update
  16.9 97.7 %reduce-scatter.5.cloned.1.call-done = f32[48,4096]{1,0:T(8,128)} async-done(((f32[768,4096]{1,0:T(8,128)}), f32[48,4096]{1,0:T(8,128)}) %reduce-scatter.5.cloned.1.call-update) | async-done | bytes 786448 | tf_op jit(solution)/shard_map/reduce_scatter | solution.py:72
  114.5 2.2 all_to_all.34
  116.7 4.4 all-to-all-start
  121.2 0.0 copy-done.1
  121.2 0.1 copy.41
  121.3 0.1 eq.29
  121.3 0.1 fusion.17
  121.4 0.1 reduce_window_sum.11
  121.5 0.2 select_reduce_fusion.1
  121.7 0.1 reduce_sum.89
  121.7 0.1 copy.42
  121.8 0.0 copy-done.3
  121.8 0.1 select_reduce_fusion
  121.9 15.2 %all-to-all-done = f32[8,6,4096]{2,1,0:T(8,128)S(1)} async-done(((f32[8,6,4096]{2,1,0:T(8,128)}), f32[8,6,4096]{2,1,0:T(8,128)S(1)}, u32[]{:S(2)}, u32[]{:S(2)}) %all-to-all-start) | async-done | bytes 786464 | tf_op jit(solution)/shard_map/all_to_all | solution.py:78
  137.1 0.1 all_to_all.36
  137.2 0.0 copy-done.2
  137.2 0.5 convolution_multiply_fusion.1
  137.7 0.8 convolution_convert_fusion.1
  138.6 0.1 all_to_all.37
  138.7 12.8 %all_to_all.52 = bf16[8,6,4096]{2,1,0:T(8,128)(2,1)S(1)} all-to-all(bf16[8,6,4096]{2,1,0:T(8,128)(2,1)S(1)} %all_to_all.37), channel_id=1, replica_groups=mesh['expert_0'=4,'expert_1'=2,'fsdp_0'=4,'fsdp_1'=4] {'expert_0','exper..., dimensions={0} | all-to-all | bytes 786432 | tf_op jit(solution)/shard_map/all_to_all | solution.py:80
  151.5 0.1 stack.8
  151.6 3.5 stack.9
  155.1 4.6 all-to-all-start.2
  159.7 0.0 reduce-scatter.7.cloned.1.call-start
  159.8 6.5 %copy.40 = bf16[1,512,4096]{1,2,0:T(8,128)(2,1)} copy(bf16[1,512,4096]{2,1,0:T(8,128)(2,1)} %param.12) | data formatting | bytes 8388608 | tf_op args[5]
  166.9 85.9 %all-to-all-done.2 = bf16[16,48,4096]{2,1,0:T(8,128)(2,1)} async-done(((bf16[16,48,4096]{2,1,0:T(8,128)(2,1)}), bf16[16,48,4096]{2,1,0:T(8,128)(2,1)}, u32[]{:S(2)}, u32[]{:S(2)}) %all-to-all-start.2) | async-done | bytes 6291488 | tf_op jit(solution)/shard_map/all_to_all | solution.py:84
  252.8 12.3 %multiply_reduce_fusion = (f32[]{:T(128)}, f32[]{:T(128)}, f32[]{:T(128)}, f32[1,512,4096]{1,2,0:T(8,128)}) fusion(bf16[1,512,4096]{1,2,0:T(8,128)(2,1)} %copy.40, f32[]{:T(128)} %bitcast.46, bf16[768,4096]{1,0:T(8,128)(2,1)} %bitcast.2, bf16[1,768,512]{2,1,0:T(8,128)(2,1)S(1)} %copy-done), kind=kOutput, calls=%fused_computation.18 | convolution fusion | flops 3240099840 | bytes 19660816 | tf_op jit(solution)/shard_map/dot_general | solution.py:81
  265.0 9.6 %all-reduce.5 = (f32[]{:T(128)}, f32[]{:T(128)}, f32[]{:T(128)}) all-reduce(f32[]{:T(128)} %get-tuple-element.17, f32[]{:T(128)} %get-tuple-element.16, f32[]{:T(128)} %get-tuple-element.15), channel_id=1, replica_groups=mesh['expert_0'=4,'expert_1'=2,'fsdp_0'=4,'fsdp_1'=4] {'expert_0'}, use_global_device_ids=true, to_apply=%region_1.2 | all-reduce | flops 3 | bytes 24 | tf_op jit(solution)/shard_map/psum | solution.py:17
  274.6 3.1 all-reduce.7
  277.8 10.8 %all-reduce.3 = (f32[]{:T(128)}, f32[]{:T(128)}, f32[]{:T(128)}) all-reduce(f32[]{:T(128)} %get-tuple-element.43, f32[]{:T(128)} %get-tuple-element.44, f32[]{:T(128)} %get-tuple-element.45), channel_id=1, replica_groups=mesh['expert_0'=4,'expert_1'=2,'fsdp_0'=4,'fsdp_1'=4] {'fsdp_0'}, use_global_device_ids=true, to_apply=%region_3.4 | all-reduce | flops 3 | bytes 24 | tf_op jit(solution)/shard_map/psum | solution.py:17
  288.5 9.6 %all-reduce.1 = (f32[]{:T(128)}, f32[]{:T(128)}, f32[]{:T(128)}) all-reduce(f32[]{:T(128)} %get-tuple-element.29, f32[]{:T(128)} %get-tuple-element.30, f32[]{:T(128)} %get-tuple-element.31), channel_id=1, replica_groups=mesh['expert_0'=4,'expert_1'=2,'fsdp_0'=4,'fsdp_1'=4] {'fsdp_1'}, use_global_device_ids=true, to_apply=%region_4.5 | all-reduce | flops 3 | bytes 24 | tf_op jit(solution)/shard_map/psum | solution.py:17
  302.0 13.1 %convolution_bitcast_fusion = f32[768,4096]{0,1:T(8,128)} fusion(bf16[1,768,512]{2,1,0:T(8,128)(2,1)S(1)} %copy-done, bf16[1,512,4096]{1,2,0:T(8,128)(2,1)} %copy.40, f32[1,512,4096]{1,2,0:T(8,128)} %get-tuple-element.46, f32[]{:T(128)S(6)} %div.13, f32[]{:T(128)S(6)} %div.12), kind=kOutput, calls=%fused_computation.20 | convolution fusion | flops 3233808384 | bytes 25952264 | tf_op jit(solution)/shard_map/dot_general | solution.py:73
  315.1 12.6 %copy.46 = f32[768,4096]{1,0:T(8,128)} copy(f32[768,4096]{0,1:T(8,128)} %convolution_bitcast_fusion) | data formatting | bytes 25165824
  327.7 0.0 reduce-scatter.7.cloned.1.call-update
  327.7 89.9 %reduce-scatter.7.cloned.1.call-done = f32[48,4096]{1,0:T(8,128)} async-done(((f32[768,4096]{1,0:T(8,128)}), f32[48,4096]{1,0:T(8,128)}) %reduce-scatter.7.cloned.1.call-update) | async-done | bytes 786448 | tf_op jit(solution)/shard_map/reduce_scatter | solution.py:72
  417.6 1.2 all_to_all.40
  418.8 20.2 %all_to_all.53 = f32[8,6,4096]{2,1,0:T(8,128)S(1)} all-to-all(f32[8,6,4096]{2,1,0:T(8,128)S(1)} %all_to_all.40), channel_id=1, replica_groups=mesh['expert_0'=4,'expert_1'=2,'fsdp_0'=4,'fsdp_1'=4] {'expert_0','exper..., dimensions={0} | all-to-all | bytes 1572864 | tf_op jit(solution)/shard_map/all_to_all | solution.py:78
  439.0 0.1 all_to_all.42
  439.2 0.5 convolution_multiply_fusion
  439.7 0.8 convolution_convert_fusion
  440.5 0.1 all_to_all.43
  440.6 12.8 %all_to_all.54 = bf16[8,6,4096]{2,1,0:T(8,128)(2,1)S(1)} all-to-all(bf16[8,6,4096]{2,1,0:T(8,128)(2,1)S(1)} %all_to_all.43), channel_id=1, replica_groups=mesh['expert_0'=4,'expert_1'=2,'fsdp_0'=4,'fsdp_1'=4] {'expert_0','exper..., dimensions={0} | all-to-all | bytes 786432 | tf_op jit(solution)/shard_map/all_to_all | solution.py:80
  453.4 0.1 stack.10
  453.5 3.4 stack.11
  457.0 4.6 all-to-all-start.5
  461.6 6.5 %copy.44 = bf16[1,512,4096]{1,2,0:T(8,128)(2,1)} copy(bf16[1,512,4096]{2,1,0:T(8,128)(2,1)} %param.13) | data formatting | bytes 8388608 | tf_op args[6]
  468.1 8.2 %fusion = (f32[]{:T(128)}, f32[]{:T(128)}, f32[]{:T(128)}) fusion(bf16[1,512,4096]{1,2,0:T(8,128)(2,1)} %copy.44, f32[]{:T(128)S(6)} %div.13, f32[1,512,4096]{1,2,0:T(8,128)} %get-tuple-element.46, f32[]{:T(128)S(6)} %div.12, bf16[1,512,4096]{1,2,0:T(8,128)(2,1)} %copy.40), kind=kLoop, calls=%fused_computation.8 | loop fusion | flops 25165824 | bytes 16777236 | tf_op jit(solution)/shard_map/reduce_sum | solution.py:51
  476.3 78.4 %all-to-all-done.5 = bf16[16,48,4096]{2,1,0:T(8,128)(2,1)} async-done(((bf16[16,48,4096]{2,1,0:T(8,128)(2,1)}), bf16[16,48,4096]{2,1,0:T(8,128)(2,1)}, u32[]{:S(2)}, u32[]{:S(2)}) %all-to-all-start.5) | async-done | bytes 6291488 | tf_op jit(solution)/shard_map/all_to_all | solution.py:84
  554.7 10.2 %fusion.8 = f32[]{:T(128)} fusion(bf16[768,4096]{1,0:T(8,128)(2,1)} %bitcast.8, f32[]{:T(128)} %bitcast.47, bf16[1,768,512]{2,1,0:T(8,128)(2,1)S(1)} %copy-done, f32[]{:T(128)S(6)} %div.13, f32[1,512,4096]{1,2,0:T(8,128)} %get-tuple-element.46, f32[]{:T(128)S(6)} %div.12, bf16[1,512,4096]{1,2,0:T(8,128)(2,1)} %copy.40), kind=kOutput, calls=%fused_computation.17 | convolution fusion | flops 3240099840 | bytes 19660816 | tf_op jit(solution)/shard_map/dot_general | solution.py:81
  564.8 9.6 %all-reduce.4 = (f32[]{:T(128)}, f32[]{:T(128)}, f32[]{:T(128)}, f32[]{:T(128)}) all-reduce(f32[]{:T(128)} %get-tuple-element.13, f32[]{:T(128)} %fusion.8, f32[]{:T(128)} %get-tuple-element.14, f32[]{:T(128)} %get-tuple-element.12), channel_id=1, replica_groups=mesh['expert_0'=4,'expert_1'=2,'fsdp_0'=4,'fsdp_1'=4] {'expert_0'}, use_global_device_ids=true, to_apply=%region_15.16 | all-reduce | flops 4 | bytes 32 | tf_op jit(solution)/shard_map/psum | solution.py:17
  574.4 3.2 all-reduce.6
  577.6 10.8 %all-reduce.2 = (f32[]{:T(128)}, f32[]{:T(128)}, f32[]{:T(128)}, f32[]{:T(128)}) all-reduce(f32[]{:T(128)} %get-tuple-element.39, f32[]{:T(128)} %get-tuple-element.40, f32[]{:T(128)} %get-tuple-element.41, f32[]{:T(128)} %get-tuple-element.42), channel_id=1, replica_groups=mesh['expert_0'=4,'expert_1'=2,'fsdp_0'=4,'fsdp_1'=4] {'fsdp_0'}, use_global_device_ids=true, to_apply=%region_17.18 | all-reduce | flops 4 | bytes 32 | tf_op jit(solution)/shard_map/psum | solution.py:17
  588.3 9.5 %all-reduce = (f32[]{:T(128)}, f32[]{:T(128)}, f32[]{:T(128)}, f32[]{:T(128)}) all-reduce(f32[]{:T(128)} %get-tuple-element.25, f32[]{:T(128)} %get-tuple-element.26, f32[]{:T(128)} %get-tuple-element.27, f32[]{:T(128)} %get-tuple-element.28), channel_id=1, replica_groups=mesh['expert_0'=4,'expert_1'=2,'fsdp_0'=4,'fsdp_1'=4] {'fsdp_1'}, use_global_device_ids=true, to_apply=%region_18.19 | all-reduce | flops 4 | bytes 32 | tf_op jit(solution)/shard_map/psum | solution.py:17
  599.2 7.7 %fusion.4 = f32[1,512,4096]{1,2,0:T(8,128)} fusion(bf16[1,512,4096]{1,2,0:T(8,128)(2,1)} %copy.40, f32[]{:T(128)S(6)} %div.14, f32[]{:T(128)S(6)} %div.12, f32[]{:T(128)S(6)} %div.13, f32[1,512,4096]{1,2,0:T(8,128)} %get-tuple-element.46), kind=kLoop, calls=%fused_computation.12 | loop fusion | flops 16777216 | bytes 20971532 | tf_op jit(solution)/shard_map/add | solution.py:92
  608.1 8.9 %copy.45 = f32[1,512,4096]{2,1,0:T(8,128)} copy(f32[1,512,4096]{1,2,0:T(8,128)} %fusion.4) | data formatting | bytes 16777216
  (1 shorter events, 0.0 us)
Async XLA Ops:
  7.2 1.1 copy-start
  7.2 107.4 %reduce-scatter.5.cloned.1.call-start = ((), (), s32[]{:S(2)}) async-start(), calls=%async_computation.8 | async-start | bytes 13369344 | tf_op jit(solution)/shard_map/reduce_scatter | solution.py:72
  16.9 104.3 %copy-start.1 = (s32[16,2]{0,1:T(2,128)S(1)}, s32[16,2]{0,1:T(2,128)}, u32[]{:S(2)}) copy-start(s32[16,2]{0,1:T(2,128)} %param.8) | copy-start | bytes 388
  16.9 105.0 %copy-start.3 = (f32[16,2]{0,1:T(2,128)S(1)}, f32[16,2]{0,1:T(2,128)}, u32[]{:S(2)}) copy-start(f32[16,2]{0,1:T(2,128)} %param.9) | copy-start | bytes 388
  16.9 120.4 %copy-start.2 = (f32[16]{0:T(128)S(1)}, f32[16]{0:T(128)}, u32[]{:S(2)}) copy-start(f32[16]{0:T(128)} %param.10) | copy-start | bytes 196
  116.7 20.4 %all-to-all-start = ((f32[8,6,4096]{2,1,0:T(8,128)}), f32[8,6,4096]{2,1,0:T(8,128)S(1)}, u32[]{:S(2)}, u32[]{:S(2)}) async-start(f32[8,6,4096]{2,1,0:T(8,128)} %all_to_all.34), calls=%async_computation.1 | async-start | bytes 2097152 | tf_op jit(solution)/shard_map/all_to_all | solution.py:78
  155.1 97.7 %all-to-all-start.2 = ((bf16[16,48,4096]{2,1,0:T(8,128)(2,1)}), bf16[16,48,4096]{2,1,0:T(8,128)(2,1)}, u32[]{:S(2)}, u32[]{:S(2)}) async-start(bf16[16,48,4096]{2,1,0:T(8,128)(2,1)} %stack.9), calls=%async_computation.3 | async-start | bytes 12582912 | tf_op jit(solution)/shard_map/all_to_all | solution.py:84
  159.7 257.9 %reduce-scatter.7.cloned.1.call-start = ((), (), s32[]{:S(2)}) async-start(), calls=%async_computation.9 | async-start | bytes 13369344 | tf_op jit(solution)/shard_map/reduce_scatter | solution.py:72
  457.0 97.7 %all-to-all-start.5 = ((bf16[16,48,4096]{2,1,0:T(8,128)(2,1)}), bf16[16,48,4096]{2,1,0:T(8,128)(2,1)}, u32[]{:S(2)}, u32[]{:S(2)}) async-start(bf16[16,48,4096]{2,1,0:T(8,128)(2,1)} %stack.11), calls=%async_computation.6 | async-start | bytes 12582912 | tf_op jit(solution)/shard_map/all_to_all | solution.py:84
Sparse Core Ops, SparseCore 0:
  17.0 97.4 reduce-scatter.4
  327.9 89.7 reduce-scatter.6
